TPU v7x, 512 devices: a 8x2x16 block of a 8x8x16 slice. The times are simulated.
512 devices in a mesh: grp: 2 (over y), seq: 128 (over x, z), bat: 2 (over core).
Axes of the slice: x: 8, y: 2, z: 16, core: 2. Of those that a mesh axis runs over, the one named last changes fastest.
The devices are a block of a 8x8x16 slice.
Arguments:
- queries: bfloat16 [16, 16, 192], P(('grp', 'bat')), parts along dimension 0, may hold values from -8 to 8
- latent_cache: bfloat16 [16, 65536, 576], P('grp', 'seq'), parts along dimension 0, may hold values from -128 to 128
- cache_lengths: int32 [16], P('grp'), parts along dimension 0, may hold values from 128 to 65536, as said below
- key_weight: bfloat16 [16, 128, 512], P('bat'), may hold values from -0.5 to 0.5
- value_weight: bfloat16 [16, 512, 128], P('bat'), may hold values from -0.25 to 0.25
Outputs:
- attended: bfloat16 [16, 16, 128], P(('grp', 'bat')), parts along dimension 0
There are 2 independent parts, one for each index of `grp`. A program takes and returns all parts, laid end to end along the dimension named above; an argument that names none is the same for every part. Nothing has to cross between parts.
Inputs may be any that keep to these rules, and one draw needn't show every extreme that they name: `cache_lengths`: each entry is a multiple of 128; at least one request has all 65536 positions valid and at least one has fewer.
All inputs are finite; a program needn't handle non-finite values.
Results may differ from a plain program's by a relative error of at most 0.0085.
Values may be sent and summed in bfloat16 or wider, within the bound.
No kernel may reach another device: no remote copies, remote signals or barrier semaphores. Data moves between devices by JAX's collectives and lax.ppermute only.
A program may use at most 64 MiB of HBM per device.

v0:
```python
import jax
import jax.numpy as jnp
from jax import lax
from jax.sharding import Mesh
from jax.sharding import PartitionSpec as P

SEQ = ("seq_0", "seq_1")


masked_score = -1e30


def gathered_once(shard, axis):
    leaves = jax.tree.leaves(shard)
    order = sorted(range(len(leaves)), key=lambda k: -leaves[k].size)
    width = (1, *leaves[order[0]].shape)[-1]
    lines = [
        jnp.pad(leaves[k].reshape(-1), (0, -leaves[k].size % width)).reshape(-1, width)
        for k in order
    ]
    both, at, found = (lax.all_gather(jnp.concatenate(lines), axis), 0, {})
    for k, line in zip(order, lines):
        piece = both[:, at : at + len(line)].reshape(len(both), -1)
        found[k] = piece[:, : leaves[k].size].reshape(-1, *leaves[k].shape)
        at += len(line)
    numbers = iter(range(len(leaves)))
    return jax.tree.map(lambda _: found[next(numbers)], shard)


def merged_by_axis(shard, axes, combine):
    for axis in axes:
        pieces = gathered_once(shard, axis)
        shard = jax.tree.map(lambda part: part[0], pieces)
        for k in range(1, lax.axis_size(axis)):
            shard = combine(shard, jax.tree.map(lambda part: part[k], pieces))
    return shard


def merge_pair(first_part, second_part):
    max_first, total_first, sums_first = first_part
    max_second, total_second, sums_second = second_part
    highest = jnp.maximum(max_first, max_second)
    factor_first = jnp.exp(max_first - highest)
    factor_second = jnp.exp(max_second - highest)
    merged_total = total_first * factor_first + total_second * factor_second
    merged_sums = sums_first * factor_first[..., None] + sums_second * factor_second[..., None]
    return (highest, merged_total, merged_sums)


def attend(joined, cache_rows, lengths, scaling, latent_width):
    scores = (
        jnp.einsum("bhc,bsc->bhs", joined, cache_rows, preferred_element_type=jnp.float32) * scaling
    )
    shard_len = cache_rows.shape[1]
    positions = lax.axis_index(SEQ) * shard_len + jnp.arange(shard_len, dtype=jnp.int32)
    usable = positions[None, :] < lengths[:, None]
    scores = jnp.where(usable[:, None, :], scores, masked_score)
    maxima = jnp.max(scores, axis=2)
    weights = jnp.exp(scores - maxima[..., None])
    totals = jnp.sum(weights, axis=2)
    rounded_weights = weights.astype(jnp.bfloat16)
    latent_sums = jnp.einsum(
        "bhs,bsc->bhc",
        rounded_weights,
        cache_rows[:, :, :latent_width],
        preferred_element_type=jnp.float32,
    )
    return (maxima, totals, latent_sums)


def per_device(queries, latent_cache, cache_lengths, key_weight, value_weight):
    nope_width = key_weight.shape[1]
    latent_width = key_weight.shape[2]
    grouped = lax.all_to_all(queries, "bat", split_axis=1, concat_axis=0, tiled=True)
    absorbed = jnp.einsum(
        "bhd,hdc->bhc", grouped[:, :, :nope_width], key_weight, preferred_element_type=jnp.float32
    ).astype(jnp.bfloat16)
    joined = jnp.concatenate([absorbed, grouped[:, :, nope_width:]], axis=2)
    scaling = queries.shape[2] ** (-0.5)
    value_full = value_weight.astype(jnp.float32)
    maxima, totals, latent_sums = attend(joined, latent_cache, cache_lengths, scaling, latent_width)
    projected = jnp.einsum("bhc,hcd->bhd", latent_sums, value_full)
    maxima, totals, projected = merged_by_axis((maxima, totals, projected), SEQ, merge_pair)
    result = projected / totals[..., None]
    result = result.astype(jnp.bfloat16)
    return lax.all_to_all(result, "bat", split_axis=0, concat_axis=1, tiled=True)


def solution(mesh):
    torus = Mesh(
        mesh.devices.reshape(mesh.shape["grp"], 8, 16, mesh.shape["bat"]),
        ("grp", "seq_0", "seq_1", "bat"),
    )
    placed = (
        P(("grp", "bat"), None, None),
        P("grp", SEQ, None),
        P("grp"),
        P("bat", None, None),
        P("bat", None, None),
    )
    return jax.shard_map(
        per_device,
        mesh=torus,
        in_specs=placed,
        out_specs=P(("grp", "bat"), None, None),
        check_vma=False,
    )
```

profile of v0, /device:TPU:80, one launch (start us, length us, event | category | flops | bytes accessed | tf_op | source)
XLA Modules:
  0.0 120.3 jit_solution(1907695189759258873)
XLA Ops:
  0.0 1.5 %copy.15 = bf16[4,16,192]{2,0,1:T(4,128)(2,1)} copy(bf16[4,16,192]{2,1,0:T(8,128)(2,1)} %param.5) | data formatting | bytes 49152 | tf_op args[0]
  1.5 3.3 %all-to-all-start = ((bf16[4,16,192]{2,0,1:T(4,128)(2,1)}), bf16[4,16,192]{2,0,1:T(4,128)(2,1)S(1)}, u32[]{:S(2)}, u32[]{:S(2)}) async-start(bf16[4,16,192]{2,0,1:T(4,128)(2,1)} %copy.15), calls=%async_computation | async-start | bytes 65536 | tf_op jit(solution)/shard_map/all_to_all | solution.py:74
  4.8 1.3 %all-to-all-done = bf16[4,16,192]{2,0,1:T(4,128)(2,1)S(1)} async-done(((bf16[4,16,192]{2,0,1:T(4,128)(2,1)}), bf16[4,16,192]{2,0,1:T(4,128)(2,1)S(1)}, u32[]{:S(2)}, u32[]{:S(2)}) %all-to-all-start) | async-done | bytes 24608 | tf_op jit(solution)/shard_map/all_to_all | solution.py:74
  6.2 0.2 fusion.3
  6.4 0.7 broadcast_compare_fusion
  7.2 3.2 %fusion.114 = (f32[8,8]{1,0:T(8,128)S(1)}, f32[8,8,512]{2,1,0:T(8,128)S(1)}) fusion(bf16[8,512,576]{1,2,0:T(8,128)(2,1)} %param.6, bf16[8,8,576]{2,0,1:T(8,128)(2,1)S(1)} %pad_maximum_fusion, pred[8,512]{1,0:T(8,128)(4,1)S(1)} %broadcast_compare_fusion), kind=kOutput, calls=%fused_computation.241 | convolution fusion | flops 37846976 | bytes 4927744 | tf_op jit(solution)/shard_map/bhc,bsc->bhs/dot_general | solution.py:52
  10.4 0.1 reshape.1692
  10.5 0.2 fusion.5
  10.7 3.4 %fusion = bf16[8,8,512]{2,1,0:T(8,128)(2,1)S(1)} fusion(bf16[8,512,576]{1,2,0:T(8,128)(2,1)} %param.6, f32[8,8,512]{2,1,0:T(8,128)S(1)} %get-tuple-element.99, f32[8,8]{1,0:T(8,128)S(1)} %get-tuple-element.98), kind=kOutput, calls=%fused_computation | convolution fusion | flops 33619968 | bytes 4391168 | tf_op jit(solution)/shard_map/bhs,bsc->bhc/dot_general | solution.py:62
  14.1 0.1 reshape.1694
  14.2 0.3 convolution_bitcast_fusion
  14.5 26.8 %all-gather.2 = f32[8,66,128]{2,1,0:T(8,128)S(1)} all-gather(f32[1,66,128]{2,1,0:T(8,128)S(1)} %maximum_bitcast_fusion), channel_id=2, replica_groups=mesh['grp'=2,'seq_0'=8,'seq_1'=16,'bat'=2] {'seq_0'}, dimensions={0}, use_global_device_ids=true | all-gather | bytes 304128 | tf_op jit(solution)/shard_map/all_gather | solution.py:21
  41.4 0.2 fusion.57
  41.6 71.2 %all-gather.3 = f32[16,66,128]{2,1,0:T(8,128)S(1)} all-gather(f32[1,66,128]{2,1,0:T(8,128)S(1)} %maximum_bitcast_fusion.1), channel_id=3, replica_groups=mesh['grp'=2,'seq_0'=8,'seq_1'=16,'bat'=2] {'seq_1'}, dimensions={0}, use_global_device_ids=true | all-gather | bytes 574464 | tf_op jit(solution)/shard_map/all_gather | solution.py:21
  112.9 0.1 squeeze.268
  113.0 0.1 squeeze.272
  113.0 0.1 squeeze.266
  113.1 0.1 squeeze.264
  113.2 0.1 squeeze.262
  113.3 0.1 squeeze.260
  113.4 0.1 squeeze.258
  113.4 0.1 squeeze.256
  113.5 0.1 squeeze.254
  113.6 0.1 squeeze.252
  113.7 0.1 squeeze.250
  113.7 0.1 squeeze.248
  114.1 0.1 squeeze.241
  114.1 0.1 squeeze.270
  114.2 0.1 squeeze.287
  114.3 0.1 squeeze.286
  114.4 0.1 squeeze.285
  114.5 0.1 squeeze.284
  114.5 0.1 squeeze.283
  114.6 0.1 squeeze.282
  114.7 0.1 squeeze.281
  114.8 0.1 squeeze.280
  114.9 0.1 squeeze.279
  115.0 0.1 squeeze.278
  115.0 0.1 squeeze.277
  115.1 0.1 squeeze.276
  115.2 0.1 squeeze.275
  115.3 0.1 squeeze.274
  115.4 0.1 squeeze.273
  115.4 0.1 maximum_maximum_fusion
  115.5 0.1 multiply_add_fusion
  115.6 0.4 fusion.77
  116.0 3.7 %all_to_all.36 = bf16[8,8,128]{2,1,0:T(8,128)(2,1)S(1)} all-to-all(bf16[8,8,128]{2,1,0:T(8,128)(2,1)S(1)} %fusion.77), channel_id=1, replica_groups=mesh['grp'=2,'seq_0'=8,'seq_1'=16,'bat'=2] {'bat'}, dimensions={0} | all-to-all | bytes 32768 | tf_op jit(solution)/shard_map/all_to_all | solution.py:86
  119.7 0.6 copy.34
  (24 shorter events, 0.5 us)
Async XLA Ops:
  0.0 6.2 %copy-start = (bf16[8,128,512]{2,1,0:T(8,128)(2,1)S(1)}, bf16[8,128,512]{2,1,0:T(8,128)(2,1)}, u32[]{:S(2)}) copy-start(bf16[8,128,512]{2,1,0:T(8,128)(2,1)} %param.8) | copy-start | bytes 3145732
  1.5 4.7 %all-to-all-start = ((bf16[4,16,192]{2,0,1:T(4,128)(2,1)}), bf16[4,16,192]{2,0,1:T(4,128)(2,1)S(1)}, u32[]{:S(2)}, u32[]{:S(2)}) async-start(bf16[4,16,192]{2,0,1:T(4,128)(2,1)} %copy.15), calls=%async_computation | async-start | bytes 65536 | tf_op jit(solution)/shard_map/all_to_all | solution.py:74
  7.2 7.0 %copy-start.1 = (bf16[8,512,128]{2,1,0:T(8,128)(2,1)S(1)}, bf16[8,512,128]{2,1,0:T(8,128)(2,1)}, u32[]{:S(2)}) copy-start(bf16[8,512,128]{2,1,0:T(8,128)(2,1)} %param.9) | copy-start | bytes 3145732
where the time goes:
time: 122 us; the launch traced here: 120 us
  blocking collectives  102 us (84%)
  matrix products  7.09 us (6%)
  local copies, waits for them, and re-layouts  4.88 us (4%)
  starting transfers between devices  3.28 us (3%)
  other arithmetic  1.71 us (1%)
  waiting for transfers between devices  1.34 us (1%)
    all_gather x2, blocking collectives, gathered_once(): both, at, found = (lax.all_gather(jnp.concatenate(lines), axis), 0, {})  98 us
    all_to_all x1, blocking collectives, per_device(): lax.all_to_all(result, 'bat', split_axis=0, concat_axis=1, tiled=True)  3.74 us
    dot_general x1, matrix products, attend(): jnp.einsum('bhs,bsc->bhc', rounded_weights, cache_rows[:, :, :latent_widt...  3.38 us
    all_to_all x1, starting transfers between devices, per_device(): lax.all_to_all(queries, 'bat', split_axis=1, concat_axis=0, tiled=True)  3.28 us
    dot_general x1, matrix products, attend(): jnp.einsum('bhc,bsc->bhs', joined, cache_rows, preferred_element_type=jnp...  3.22 us
  transfers between devices with their start and end apart: 1, of which 1 were waited for; matrix products, arithmetic and copies ran while one was open for 0% of the time, Pallas kernels for 0%

commit v1 on v0

v1 whole, which is shorter than its diff:
```python
import functools

import jax
import jax.numpy as jnp
from jax import lax
from jax.experimental import pallas as pl
from jax.experimental.pallas import tpu as pltpu
from jax.sharding import Mesh
from jax.sharding import PartitionSpec as P

SEQ = ("seq_0", "seq_1")
SEQ_0 = 8
BAT = 2

masked_score = -1e30
lanes = 128
terms = 3
small_grant = 8 * 2**20
large_grant = 51 * 2**20


def split_terms(value):
    parts = []
    for _ in range(terms):
        part = value.astype(jnp.bfloat16).astype(jnp.float32)
        parts.append(part)
        value = value - part
    return parts


def put_stats(stats, k, width, maxima, totals):
    lane = lax.broadcasted_iota(jnp.int32, stats.shape, 1)
    for i, part in enumerate(split_terms(maxima) + split_terms(totals)):
        stats = jnp.where(lane == i * width + k, part, stats)
    return stats


def take_stats(stats, width):
    parts = [stats[..., i * width : (i + 1) * width] for i in range(2 * terms)]
    return (parts[0] + parts[1] + parts[2], parts[3] + parts[4] + parts[5])


def attend_kernel(scaling, lengths, start, query, cache, value, out, latent, keys, arrived):
    requests, heads = query.shape[:2]
    latent_width, shard_len = value.shape[1], cache.shape[2]
    own = requests // BAT
    copies = [
        pltpu.make_async_copy(cache.at[r], keys.at[r], arrived.at[r]) for r in range(requests)
    ]
    for copy in copies:
        copy.start()
    positions = start[0] + lax.broadcasted_iota(jnp.int32, (heads, shard_len), 1)
    stats = [jnp.zeros((heads, lanes), jnp.float32) for _ in range(BAT)]
    for r in range(requests):
        copies[r].wait()
        scores = jnp.dot(query[r], keys[r], preferred_element_type=jnp.float32) * scaling
        scores = jnp.where(positions < lengths[r], scores, masked_score)
        maxima = jnp.max(scores, axis=1, keepdims=True)
        weights = jnp.exp(scores - maxima)
        totals = jnp.sum(weights, axis=1, keepdims=True)
        latent[:, r, :] = lax.dot_general(
            weights.astype(jnp.bfloat16),
            keys[r, :latent_width],
            (((1,), (1,)), ((), ())),
            preferred_element_type=jnp.float32,
        )
        stats[r // own] = put_stats(stats[r // own], r % own, own, maxima, totals)
    projected = [
        jnp.dot(latent[h].astype(jnp.bfloat16), value[h], preferred_element_type=jnp.float32)
        for h in range(heads)
    ]
    projected = jnp.stack(projected, axis=1)
    for b in range(BAT):
        block = projected[b * own : (b + 1) * own].reshape(own * heads, lanes)
        block = jnp.concatenate([block, stats[b]], axis=0).astype(jnp.bfloat16)
        for x in range(out.shape[0]):
            out[x, b] = block


def attend(joined, cache, lengths, start, value, scaling, copies):
    requests, heads, _ = joined.shape
    turned = jnp.swapaxes(cache, 1, 2)
    vmem, smem = pl.BlockSpec(memory_space=pltpu.VMEM), pl.BlockSpec(memory_space=pltpu.SMEM)
    return pl.pallas_call(
        functools.partial(attend_kernel, scaling),
        out_shape=jax.ShapeDtypeStruct(
            (copies, BAT, (requests // BAT + 1) * heads, lanes), jnp.bfloat16
        ),
        in_specs=[smem, smem, vmem, pl.BlockSpec(memory_space=pltpu.HBM), vmem],
        out_specs=vmem,
        scratch_shapes=[
            pltpu.VMEM((heads, requests, value.shape[1]), jnp.float32),
            pltpu.VMEM(turned.shape, turned.dtype),
            pltpu.SemaphoreType.DMA((requests,)),
        ],
        compiler_params=pltpu.CompilerParams(vmem_limit_bytes=large_grant),
        name="attend",
    )(lengths, start, joined, turned, value)


def merged(tiles, stats, width):
    heads = stats.shape[1]
    maxima, totals = take_stats(stats, width)
    highest = jnp.max(maxima, axis=0, keepdims=True)
    factors = jnp.exp(maxima - highest)
    total = jnp.sum(totals * factors, axis=0)
    sums = []
    for k in range(width):
        part = tiles[:, k * heads : (k + 1) * heads] * factors[:, :, k : k + 1]
        sums.append(jnp.sum(part, axis=0))
    return sums, highest[0], total


def merge_kernel(heads, pieces, out):
    copies = out.shape[0]
    rows = pieces.shape[2]
    width = rows // heads - 1
    for b in range(BAT):
        block = pieces[:, b].astype(jnp.float32)
        sums, highest, total = merged(block[:, : width * heads], block[:, width * heads :], width)
        stats = jnp.zeros((heads, lanes), jnp.float32)
        for k in range(width):
            stats = put_stats(stats, k, width, highest[:, k : k + 1], total[:, k : k + 1])
        result = jnp.concatenate([*sums, stats], axis=0).astype(jnp.bfloat16)
        for c in range(copies):
            out[c, b] = result


def finish_kernel(heads, pieces, out):
    rows = pieces.shape[2]
    width = rows // heads - 1
    for b in range(BAT):
        block = pieces[:, b].astype(jnp.float32)
        sums, _, total = merged(block[:, : width * heads], block[:, width * heads :], width)
        for k in range(width):
            out[k, b] = (sums[k] / total[:, k : k + 1]).astype(jnp.bfloat16)


def whole(kernel, shape, name, operand):
    return pl.pallas_call(
        kernel,
        out_shape=jax.ShapeDtypeStruct(shape, jnp.bfloat16),
        in_specs=[pl.BlockSpec(memory_space=pltpu.VMEM)],
        out_specs=pl.BlockSpec(memory_space=pltpu.VMEM),
        compiler_params=pltpu.CompilerParams(vmem_limit_bytes=small_grant),
        name=name,
    )(operand)


def per_device(queries, latent_cache, cache_lengths, key_weight, value_weight):
    nope_width = key_weight.shape[1]
    heads = key_weight.shape[0]
    grouped = lax.all_to_all(queries, "bat", split_axis=1, concat_axis=0, tiled=True)
    absorbed = jnp.einsum(
        "bhd,hdc->bhc", grouped[:, :, :nope_width], key_weight, preferred_element_type=jnp.float32
    ).astype(jnp.bfloat16)
    joined = jnp.concatenate([absorbed, grouped[:, :, nope_width:]], axis=2)
    scaling = queries.shape[2] ** (-0.5)
    shard_len = latent_cache.shape[1]
    start = (lax.axis_index(SEQ) * shard_len).astype(jnp.int32).reshape(1)
    across, along = lax.axis_size("seq_0"), lax.axis_size("seq_1")
    partial = attend(joined, latent_cache, cache_lengths, start, value_weight, scaling, across)
    shape = partial.shape
    pieces = lax.all_to_all(
        partial.reshape(across * BAT, *shape[2:]), ("seq_0", "bat"), 0, 0, tiled=True
    ).reshape(shape)
    partial = whole(
        functools.partial(merge_kernel, heads), (along, *shape[1:]), "merge_across", pieces
    )
    pieces = lax.all_to_all(partial, "seq_1", 0, 0, tiled=True)
    own = queries.shape[0]
    result = whole(
        functools.partial(finish_kernel, heads),
        (own, BAT, heads, value_weight.shape[2]),
        "finish",
        pieces,
    )
    return result.reshape(own, BAT * heads, value_weight.shape[2])


def solution(mesh):
    torus = Mesh(
        mesh.devices.reshape(mesh.shape["grp"], SEQ_0, mesh.shape["seq"] // SEQ_0, mesh.shape["bat"]),
        ("grp", "seq_0", "seq_1", "bat"),
    )
    placed = (
        P(("grp", "bat"), None, None),
        P("grp", SEQ, None),
        P("grp"),
        P("bat", None, None),
        P("bat", None, None),
    )
    return jax.shard_map(
        per_device,
        mesh=torus,
        in_specs=placed,
        out_specs=P(("grp", "bat"), None, None),
        check_vma=False,
    )
```

time: 122 us -> 97.8 us (0.80); the launches traced: 120 us -> 97.4 us
  blocking collectives: 102 us -> 82 us
  Pallas kernels: 0 us -> 7.09 us
  matrix products: 7.09 us -> 0.23 us
  other arithmetic: 1.71 us -> 0.01 us
  local copies, waits for them, and re-layouts: 4.88 us -> 3.4 us
    all_gather x2 -> x0, blocking collectives: 98 us -> none  [gathered_once(): both, at, found = (lax.all_gather(jnp.concatenate(lines), axis), 0, {})]
    all_to_all x1 -> x2, blocking collectives: 3.74 us -> 82 us  [the longest x1 65.6 us: per_device(): pieces = lax.all_to_all(partial, 'seq_1', 0, 0, tiled=True)]
    pallas_call x0 -> x3, Pallas kernels: none -> 7.09 us  [the longest x1 5.68 us: attend(): pl.pallas_call(functools.partial(attend_kernel, scaling), out_shape=jax.S...]
    dot_general x3 -> x0, matrix products: 6.85 us -> none  [the longest x1 3.38 us: attend(): jnp.einsum('bhs,bsc->bhc', rounded_weights, cache_rows[:, :, :latent_widt...]
    squeeze x32 -> x0, local copies, waits for them, and re-layouts: 2.47 us -> none  [the longest x30 2.31 us: merged_by_axis(): shard = combine(shard, jax.tree.map(lambda part: part[k], pieces))]
    unnamed x5 -> x7, local copies, waits for them, and re-layouts: 1.47 us -> 3.35 us
where the time goes in v1:
time: 97.8 us; the launch traced here: 97.4 us
  blocking collectives  82 us (84%)
  Pallas kernels  7.09 us (7%)
  local copies, waits for them, and re-layouts  3.4 us (3%)
  starting transfers between devices  3.28 us (3%)
  waiting for transfers between devices  1.36 us (1%)
    all_to_all x1, blocking collectives, per_device(): pieces = lax.all_to_all(partial, 'seq_1', 0, 0, tiled=True)  65.6 us
    all_to_all x1, blocking collectives, per_device(): lax.all_to_all(partial.reshape(across * BAT, *shape[2:]), ('seq_0', 'bat'...  16.4 us
    pallas_call x1, Pallas kernels, attend(): pl.pallas_call(functools.partial(attend_kernel, scaling), out_shape=jax.S...  5.68 us
    unnamed x7, local copies, waits for them, and re-layouts  3.35 us
    all_to_all x1, starting transfers between devices, per_device(): lax.all_to_all(queries, 'bat', split_axis=1, concat_axis=0, tiled=True)  3.28 us
  transfers between devices with their start and end apart: 1, of which 1 were waited for; matrix products, arithmetic and copies ran while one was open for 0% of the time, Pallas kernels for 0%

profile of v1, /device:TPU:80, one launch (start us, length us, event | category | flops | bytes accessed | tf_op | source)
XLA Modules:
  0.0 97.4 jit_solution(3986843555691387892)
XLA Ops:
  0.0 0.0 copy-start
  0.0 1.5 %copy.9 = bf16[4,16,192]{2,0,1:T(4,128)(2,1)} copy(bf16[4,16,192]{2,1,0:T(8,128)(2,1)} %param.5) | data formatting | bytes 49152 | tf_op args[0]
  1.5 3.3 %all-to-all-start = ((bf16[4,16,192]{2,0,1:T(4,128)(2,1)}), bf16[4,16,192]{2,0,1:T(4,128)(2,1)S(1)}, u32[]{:S(2)}, u32[]{:S(2)}) async-start(bf16[4,16,192]{2,0,1:T(4,128)(2,1)} %copy.9), calls=%async_computation | async-start | bytes 65536 | tf_op jit(solution)/shard_map/all_to_all | solution.py:153
  4.8 1.4 %all-to-all-done = bf16[4,16,192]{2,0,1:T(4,128)(2,1)S(1)} async-done(((bf16[4,16,192]{2,0,1:T(4,128)(2,1)}), bf16[4,16,192]{2,0,1:T(4,128)(2,1)S(1)}, u32[]{:S(2)}, u32[]{:S(2)}) %all-to-all-start) | async-done | bytes 24608 | tf_op jit(solution)/shard_map/all_to_all | solution.py:153
  6.2 0.0 copy-done
  6.2 0.2 fusion.1
  6.5 0.0 copy-start.1
  6.5 1.2 %copy-done.1 = bf16[8,512,128]{2,1,0:T(8,128)(2,1)S(1)} copy-done((bf16[8,512,128]{2,1,0:T(8,128)(2,1)S(1)}, bf16[8,512,128]{2,1,0:T(8,128)(2,1)}, u32[]{:S(2)}) %copy-start.1) | copy-done | bytes 1048600
  7.7 0.0 copy-start.2
  7.7 0.7 copy-done.2
  8.4 5.7 %attend.1 = bf16[8,2,40,128]{3,2,1,0:T(8,128)(2,1)S(1)} custom-call(s32[8]{0:T(128)S(1)} %copy-done.2, s32[1]{0:T(128)} %bitcast.start, bf16[8,8,576]{2,1,0:T(8,128)(2,1)S(1)} %pad_maximum_fusion.query, bf16[8,576,512]{2,1,0:T(8,128)(2,1)} %bitcast.15, bf16[8,512,128]{2,1,0:T(8,128)(2,1)S(1)} %copy-done.1), custom_call_target="tpu_custom_call" | custom-call | tf_op jit(solution)/shard_map/attend/pallas_call | solution.py:84
  14.0 16.4 %all_to_all.28 = bf16[16,40,128]{2,1,0:T(8,128)(2,1)S(1)} all-to-all(bf16[16,40,128]{2,1,0:T(8,128)(2,1)S(1)} %bitcast.13), channel_id=1, replica_groups=mesh['grp'=2,'seq_0'=8,'seq_1'=16,'bat'=2] {'seq_0','bat'}, dimensions={0} | all-to-all | bytes 327680 | tf_op jit(solution)/shard_map/all_to_all | solution.py:164
  30.5 0.3 merge_across.1
  30.8 65.6 %all_to_all.29.pieces = bf16[16,2,40,128]{3,2,1,0:T(8,128)(2,1)S(1)} all-to-all(bf16[16,2,40,128]{3,2,1,0:T(8,128)(2,1)S(1)} %merge_across.1), channel_id=1, replica_groups=mesh['grp'=2,'seq_0'=8,'seq_1'=16,'bat'=2] {'seq_1'}, dimensions={0} | all-to-all | bytes 655360 | tf_op jit(solution)/shard_map/all_to_all | solution.py:170
  96.3 1.1 %finish.1 = bf16[4,2,8,128]{3,2,1,0:T(8,128)(2,1)} custom-call(bf16[16,2,40,128]{3,2,1,0:T(8,128)(2,1)S(1)} %all_to_all.29.pieces), custom_call_target="tpu_custom_call" | custom-call | tf_op jit(solution)/shard_map/finish/pallas_call | solution.py:140
  (5 shorter events, 0.1 us)
Async XLA Ops:
  0.0 6.2 %copy-start = (bf16[8,128,512]{2,1,0:T(8,128)(2,1)S(1)}, bf16[8,128,512]{2,1,0:T(8,128)(2,1)}, u32[]{:S(2)}) copy-start(bf16[8,128,512]{2,1,0:T(8,128)(2,1)} %param.8) | copy-start | bytes 3145732
  1.5 4.7 %all-to-all-start = ((bf16[4,16,192]{2,0,1:T(4,128)(2,1)}), bf16[4,16,192]{2,0,1:T(4,128)(2,1)S(1)}, u32[]{:S(2)}, u32[]{:S(2)}) async-start(bf16[4,16,192]{2,0,1:T(4,128)(2,1)} %copy.9), calls=%async_computation | async-start | bytes 65536 | tf_op jit(solution)/shard_map/all_to_all | solution.py:153
  6.5 1.2 %copy-start.1 = (bf16[8,512,128]{2,1,0:T(8,128)(2,1)S(1)}, bf16[8,512,128]{2,1,0:T(8,128)(2,1)}, u32[]{:S(2)}) copy-start(bf16[8,512,128]{2,1,0:T(8,128)(2,1)} %value.1) | copy-start | bytes 3145732
  7.7 0.7 copy-start.2
